TPU v7x, 32 devices: a whole 2x2x4 slice. The times are simulated.
32 devices in a mesh: dp: 4 (over z), tp: 8 (over y, x, core).
Axes of the slice: x: 2, y: 2, z: 4, core: 2. Of those that a mesh axis runs over, the one named last changes fastest.
Arguments:
- layer_input: bfloat16 [8192, 2048], P(('dp', 'tp')), may hold values from -6 to 6
- segments: int32 [4, 2048], P('dp'), may hold values from 0 to 1, as said below
- norm_gains: float32 [2, 2048], replicated, may hold values from 0.25 to 1.75
- norm_biases: float32 [2, 2048], replicated, may hold values from -2 to 2
- w_qkv: bfloat16 [2048, 3, 2048], P(None, None, 'tp'), may hold values from -0.125 to 0.125
- qv_bias: float32 [2, 2048], P(None, 'tp'), may hold values from -2 to 2
- key_bias: float32 [32, 16], P('tp'), may hold values from -3 to 3
- w_out: bfloat16 [2048, 2048], P('tp'), may hold values from -2 to 2
- w_gate_up: bfloat16 [2048, 2, 5632], P(None, None, 'tp'), may hold values from -0.125 to 0.125
- w_down: bfloat16 [5632, 2048], P('tp'), may hold values from -0.078125 to 0.078125
- out_grad: bfloat16 [8192, 2048], P(('dp', 'tp')), may hold values from -6 to 6
Outputs:
- output: float32 [8192, 2048], P(('dp', 'tp'))
- grad_x: float32 [8192, 2048], P(('dp', 'tp'))
- grad_qkv: float32 [2048, 3, 2048], P(None, None, 'tp')
- grad_qv_bias: float32 [2, 2048], P(None, 'tp')
- grad_key_bias: float32 [32, 16], P('tp')
- grad_out: float32 [2048, 2048], P('tp')
- grad_gate_up: float32 [2048, 2, 5632], P(None, None, 'tp')
- grad_down: float32 [5632, 2048], P('tp')
- grad_gains: float32 [2, 2048], P(None, 'tp')
- grad_biases: float32 [2, 2048], P(None, 'tp')
Inputs may be any that keep to these rules, and one draw needn't show every extreme that they name: `segments`: in each group the ids number the documents from 0 and never fall; every document has 1024 tokens or more.
All inputs are finite; a program needn't handle non-finite values.
Results may differ from a plain program's by a relative error of at most 0.023.
Values may be sent and summed in bfloat16 or wider, within the bound.
A program may use at most 256 MiB of HBM per device.

v0:
```python
import math
import jax
import jax.numpy as jnp
from jax import lax
from jax.sharding import PartitionSpec as P

D = 2048
HEAD_DIM = 64
ROT = 16
EPSILON = 1e-05


def norm_forward(values, gain, shift_bias):
    centre = jnp.mean(values, axis=-1, keepdims=True)
    centred = values - centre
    spread = jnp.mean(centred * centred, axis=-1, keepdims=True)
    inverse = lax.rsqrt(spread + EPSILON)
    normed = centred * inverse
    return (normed * gain + shift_bias, normed, inverse)


def norm_backward(grad_normed, normed, inverse, gain):
    scaled = grad_normed * gain
    inner = jnp.mean(scaled, axis=-1, keepdims=True)
    along = jnp.mean(scaled * normed, axis=-1, keepdims=True)
    return (
        inverse * (scaled - inner - normed * along),
        jnp.sum(grad_normed * normed, axis=0),
        jnp.sum(grad_normed, axis=0),
    )


def rotary_tables(segment_ids):
    places = jnp.arange(segment_ids.shape[0], dtype=jnp.int32)
    starts_here = jnp.concatenate(
        [jnp.ones((1,), dtype=jnp.bool_), segment_ids[1:] != segment_ids[:-1]]
    )
    doc_start = lax.cummax(jnp.where(starts_here, places, 0), axis=0)
    positions = (places - doc_start).astype(jnp.float32)
    halves = ROT // 2
    frequency = jnp.exp(jnp.arange(halves, dtype=jnp.float32) * (-2.0 * math.log(10000.0) / ROT))
    angles = positions[:, None] * frequency[None, :]
    return (jnp.cos(angles)[:, None, :], jnp.sin(angles)[:, None, :])


def rotate(tensor, cosine, sine):
    halves = ROT // 2
    first_half = tensor[..., :halves]
    second_half = tensor[..., halves:ROT]
    return jnp.concatenate(
        [
            first_half * cosine - second_half * sine,
            second_half * cosine + first_half * sine,
            tensor[..., ROT:],
        ],
        axis=-1,
    )


def rotate_back(tensor, cosine, sine):
    halves = ROT // 2
    first_half = tensor[..., :halves]
    second_half = tensor[..., halves:ROT]
    return jnp.concatenate(
        [
            first_half * cosine + second_half * sine,
            second_half * cosine - first_half * sine,
            tensor[..., ROT:],
        ],
        axis=-1,
    )


def contract_rows(left, right):
    return lax.dot_general(
        left, right, (((0,), (0,)), ((), ())), preferred_element_type=jnp.float32
    )


def contract_cols(left, right):
    return lax.dot_general(
        left, right, (((1,), (1,)), ((), ())), preferred_element_type=jnp.float32
    )


def local(
    layer_input,
    segments,
    norm_gains,
    norm_biases,
    w_qkv,
    qv_bias,
    key_bias,
    w_out,
    w_gate_up,
    w_down,
    out_grad,
):
    segment_ids = segments[0]
    group_rows = segment_ids.shape[0]
    local_width = w_qkv.shape[2]
    local_heads = local_width // HEAD_DIM
    local_hidden = w_down.shape[0]
    block_rows = min(512, group_rows)
    blocks = group_rows // block_rows
    scale = HEAD_DIM ** (-0.5)
    places = jnp.arange(group_rows, dtype=jnp.int32)
    cosine, sine = rotary_tables(segment_ids)
    qkv_matrix = w_qkv.reshape(D, 3 * local_width)
    gate_matrix = w_gate_up.reshape(D, 2 * local_hidden)
    x_float = layer_input.astype(jnp.float32)
    normed_one, hat_one, inverse_one = norm_forward(x_float, norm_gains[0], norm_biases[0])
    rows_one = lax.all_gather(normed_one.astype(jnp.bfloat16), "tp", axis=0, tiled=True)
    projected = jnp.dot(rows_one, qkv_matrix, preferred_element_type=jnp.float32).reshape(
        group_rows, 3, local_heads, HEAD_DIM
    )
    key_full = jnp.concatenate(
        [key_bias, jnp.zeros((local_heads, HEAD_DIM - ROT), jnp.float32)], axis=1
    )
    bias_all = jnp.stack(
        [
            qv_bias[0].reshape(local_heads, HEAD_DIM),
            key_full,
            qv_bias[1].reshape(local_heads, HEAD_DIM),
        ]
    )
    projected = projected + bias_all[None]
    queries = rotate(projected[:, 0], cosine, sine).astype(jnp.bfloat16)
    key_rows = rotate(projected[:, 1], cosine, sine).astype(jnp.bfloat16)
    value_rows = projected[:, 2].astype(jnp.bfloat16)
    query_blocks = queries.reshape(blocks, block_rows, local_heads, HEAD_DIM)
    segment_blocks = segment_ids.reshape(blocks, block_rows)
    place_blocks = places.reshape(blocks, block_rows)

    def scores_of(query_block, segment_block, place_block):
        raw = (
            jnp.einsum("bhd,khd->hbk", query_block, key_rows, preferred_element_type=jnp.float32)
            * scale
        )
        visible = (segment_block[:, None] == segment_ids[None, :]) & (
            place_block[:, None] >= places[None, :]
        )
        return jnp.where(visible[None], raw, -jnp.inf)

    def forward_block(item):
        query_block, segment_block, place_block = item
        scores = scores_of(query_block, segment_block, place_block)
        highest = jnp.max(scores, axis=-1, keepdims=True)
        expo = jnp.exp(scores - highest)
        totals = jnp.sum(expo, axis=-1, keepdims=True)
        probs = (expo / totals).astype(jnp.bfloat16)
        mixed = jnp.einsum("hbk,khd->bhd", probs, value_rows, preferred_element_type=jnp.float32)
        return (mixed.astype(jnp.bfloat16), (highest + jnp.log(totals))[..., 0])

    attended, log_totals = lax.map(forward_block, (query_blocks, segment_blocks, place_blocks))
    attended = attended.reshape(group_rows, local_width)
    hidden_state = x_float + lax.psum_scatter(
        jnp.dot(attended, w_out, preferred_element_type=jnp.float32).astype(jnp.bfloat16),
        "tp",
        scatter_dimension=0,
        tiled=True,
    ).astype(jnp.float32)
    normed_two, hat_two, inverse_two = norm_forward(hidden_state, norm_gains[1], norm_biases[1])
    rows_two = lax.all_gather(normed_two.astype(jnp.bfloat16), "tp", axis=0, tiled=True)
    gate_up = jnp.dot(rows_two, gate_matrix, preferred_element_type=jnp.float32).reshape(
        group_rows, 2, local_hidden
    )
    gate_part = gate_up[:, 0]
    up_part = gate_up[:, 1]
    sigmoid_gate = jax.nn.sigmoid(gate_part)
    silu_gate = gate_part * sigmoid_gate
    activation = (silu_gate * up_part).astype(jnp.bfloat16)
    output = hidden_state + lax.psum_scatter(
        jnp.dot(activation, w_down, preferred_element_type=jnp.float32).astype(jnp.bfloat16),
        "tp",
        scatter_dimension=0,
        tiled=True,
    ).astype(jnp.float32)
    grad_float = out_grad.astype(jnp.float32)
    portion = lax.all_gather(out_grad, "tp", axis=0, tiled=True)
    weight_sum = contract_rows(activation, portion)
    grad_act = contract_cols(portion, w_down)
    grad_down, grad_act = (weight_sum, grad_act)
    grad_gate = grad_act * up_part * sigmoid_gate * (1.0 + gate_part * (1.0 - sigmoid_gate))
    grad_up = grad_act * silu_gate
    grad_pair = (
        jnp.stack([grad_gate, grad_up], axis=1)
        .astype(jnp.bfloat16)
        .reshape(group_rows, 2 * local_hidden)
    )
    grad_gate_up = contract_rows(rows_two, grad_pair).reshape(D, 2, local_hidden)
    grad_normed_two = lax.psum_scatter(
        contract_cols(grad_pair, gate_matrix).astype(jnp.bfloat16),
        "tp",
        scatter_dimension=0,
        tiled=True,
    ).astype(jnp.float32)
    back_two, gain_two, shift_two = norm_backward(
        grad_normed_two, hat_two, inverse_two, norm_gains[1]
    )
    grad_hidden = grad_float + back_two
    portion = lax.all_gather(grad_hidden.astype(jnp.bfloat16), "tp", axis=0, tiled=True)
    weight_sum = contract_rows(attended, portion)
    grad_att = contract_cols(portion, w_out)
    grad_out = weight_sum
    grad_blocks = grad_att.astype(jnp.bfloat16).reshape(blocks, block_rows, local_heads, HEAD_DIM)

    def backward_block(running, item):
        grad_keys, grad_values = running
        query_block, grad_block, log_block, segment_block, place_block = item
        scores = scores_of(query_block, segment_block, place_block)
        weights = jnp.exp(scores - log_block[..., None])
        grad_values = grad_values + jnp.einsum(
            "hbk,bhd->khd",
            weights.astype(jnp.bfloat16),
            grad_block,
            preferred_element_type=jnp.float32,
        )
        grad_weights = jnp.einsum(
            "bhd,khd->hbk", grad_block, value_rows, preferred_element_type=jnp.float32
        )
        inner = jnp.sum(weights * grad_weights, axis=-1, keepdims=True)
        grad_scores = (weights * (grad_weights - inner)).astype(jnp.bfloat16)
        grad_query = (
            jnp.einsum("hbk,khd->bhd", grad_scores, key_rows, preferred_element_type=jnp.float32)
            * scale
        )
        grad_keys = (
            grad_keys
            + jnp.einsum(
                "hbk,bhd->khd", grad_scores, query_block, preferred_element_type=jnp.float32
            )
            * scale
        )
        return ((grad_keys, grad_values), grad_query)

    zero_heads = jnp.zeros((group_rows, local_heads, HEAD_DIM), jnp.float32)
    (grad_keys, grad_values), grad_queries = lax.scan(
        backward_block,
        (zero_heads, zero_heads),
        (query_blocks, grad_blocks, log_totals, segment_blocks, place_blocks),
    )
    grad_queries = grad_queries.reshape(group_rows, local_heads, HEAD_DIM)
    grad_projected = jnp.stack(
        [
            rotate_back(grad_queries, cosine, sine),
            rotate_back(grad_keys, cosine, sine),
            grad_values,
        ],
        axis=1,
    ).astype(jnp.bfloat16)
    bias_sums = jnp.sum(grad_projected, axis=0, dtype=jnp.float32)
    grad_qv = jnp.stack([bias_sums[0].reshape(local_width), bias_sums[2].reshape(local_width)])
    grad_key = bias_sums[1][:, :ROT]
    grad_flat = grad_projected.reshape(group_rows, 3 * local_width)
    grad_qkv = contract_rows(rows_one, grad_flat).reshape(D, 3, local_width)
    grad_normed_one = lax.psum_scatter(
        contract_cols(grad_flat, qkv_matrix).astype(jnp.bfloat16),
        "tp",
        scatter_dimension=0,
        tiled=True,
    ).astype(jnp.float32)
    back_one, gain_one, shift_one = norm_backward(
        grad_normed_one, hat_one, inverse_one, norm_gains[0]
    )
    grad_input = grad_hidden + back_one
    gain_grads, shift_grads = (
        lax.psum_scatter(
            jnp.stack([gain_one, gain_two]).astype(jnp.bfloat16),
            "tp",
            scatter_dimension=1,
            tiled=True,
        ).astype(jnp.float32),
        lax.psum_scatter(
            jnp.stack([shift_one, shift_two]).astype(jnp.bfloat16),
            "tp",
            scatter_dimension=1,
            tiled=True,
        ).astype(jnp.float32),
    )
    grad_qkv, grad_qv, grad_key, grad_out, grad_gate_up, grad_down, gain_grads, shift_grads = (
        lax.psum(grad_qkv.astype(jnp.bfloat16), "dp").astype(jnp.float32),
        lax.psum(grad_qv.astype(jnp.bfloat16), "dp").astype(jnp.float32),
        lax.psum(grad_key.astype(jnp.bfloat16), "dp").astype(jnp.float32),
        lax.psum(grad_out.astype(jnp.bfloat16), "dp").astype(jnp.float32),
        lax.psum(grad_gate_up.astype(jnp.bfloat16), "dp").astype(jnp.float32),
        lax.psum(grad_down.astype(jnp.bfloat16), "dp").astype(jnp.float32),
        lax.psum(gain_grads.astype(jnp.bfloat16), "dp").astype(jnp.float32),
        lax.psum(shift_grads.astype(jnp.bfloat16), "dp").astype(jnp.float32),
    )
    return (
        output,
        grad_input,
        grad_qkv,
        grad_qv,
        grad_key,
        grad_out,
        grad_gate_up,
        grad_down,
        gain_grads,
        shift_grads,
    )


def solution(mesh):
    in_specs = (
        P(("dp", "tp"), None),
        P("dp", None),
        P(),
        P(),
        P(None, None, "tp"),
        P(None, "tp"),
        P("tp", None),
        P("tp", None),
        P(None, None, "tp"),
        P("tp", None),
        P(("dp", "tp"), None),
    )
    out_specs = (
        P(("dp", "tp"), None),
        P(("dp", "tp"), None),
        P(None, None, "tp"),
        P(None, "tp"),
        P("tp", None),
        P("tp", None),
        P(None, None, "tp"),
        P("tp", None),
        P(None, "tp"),
        P(None, "tp"),
    )
    return jax.shard_map(local, mesh=mesh, in_specs=in_specs, out_specs=out_specs, check_vma=False)
```

profile of v0, /device:TPU:0, one launch (start us, length us, event | category | flops | bytes accessed | tf_op | source)
XLA Modules:
  0.0 1480.7 jit_solution(10848038059797148822)
XLA Ops:
  23.3 49.9 %all-gather.5.cloned.1.call-done = bf16[2048,2048]{1,0:T(8,128)(2,1)} async-done(((bf16[256,2048]{1,0:T(8,128)(2,1)}), bf16[2048,2048]{1,0:T(8,128)(2,1)}) %all-gather.5.cloned.1.call-update) | async-done | bytes 8388624 | tf_op jit(solution)/shard_map/all_gather | solution.py:113
  73.2 10.1 fusion.63
  88.5 63.9 %while.28 = (s32[]{:T(128)}, bf16[4,512,4,64]{1,3,2,0:T(8,128)(2,1)}, f32[4,4,512]{2,1,0:T(4,128)S(1)}, s32[4,512]{1,0:T(4,128)S(1)}, s32[1,2048]{1,0:T(1,128)S(...) while((s32[]{:T(128)}, ...), condition=%wide.region_7.8_spmd.clone, body=%wide.region_4.7_spmd.clone.sunk | while | flops 1127348224 | bytes 61427864 | solution.py:155
  98.5 5.9 fusion.150
  114.4 5.9 fusion.150
  130.3 5.9 fusion.150
  146.3 5.9 fusion.150
  155.8 5.8 convolution_convert_fusion.2
  161.7 71.6 %reduce-scatter.11.cloned.1.call-done = bf16[256,2048]{1,0:T(8,128)(2,1)} async-done(((bf16[2048,2048]{1,0:T(8,128)(2,1)}), bf16[256,2048]{1,0:T(8,128)(2,1)}) %reduce-scatter.11.cloned.1.call-update) | async-done | bytes 1048592 | tf_op jit(solution)/shard_map/reduce_scatter | solution.py:157
  239.6 53.8 %all-gather.7.cloned.1.call-done = bf16[2048,2048]{1,0:T(8,128)(2,1)} async-done(((bf16[256,2048]{1,0:T(8,128)(2,1)}), bf16[2048,2048]{1,0:T(8,128)(2,1)}) %all-gather.7.cloned.1.call-update) | async-done | bytes 8388624 | tf_op jit(solution)/shard_map/all_gather | solution.py:164
  293.4 18.8 %fusion.53 = f32[2048,2,704]{0,2,1:T(8,128)} fusion(bf16[2048,2048]{1,0:T(8,128)(2,1)} %all-gather.7.cloned.1.call-done, bf16[2048,2,704]{0,2,1:T(8,128)(2,1)} %param.23), kind=kOutput, calls=%fused_computation.64 | convolution fusion | flops 11811160064 | bytes 25690112 | tf_op jit(solution)/shard_map/dot_general | solution.py:165
  312.2 37.2 %all-gather.9.cloned.1.call-done = bf16[2048,2048]{1,0:T(8,128)(2,1)} async-done(((bf16[256,2048]{1,0:T(8,128)(2,1)}), bf16[2048,2048]{1,0:T(8,128)(2,1)}) %all-gather.9.cloned.1.call-update) | async-done | bytes 8388624 | tf_op jit(solution)/shard_map/all_gather | solution.py:180
  349.4 12.9 multiply_bitcast_fusion.1
  364.9 17.9 %bitcast_convert_fusion = bf16[2048,2048]{1,0:T(8,128)(2,1)} fusion(bf16[2048,2,704]{0,2,1:T(8,128)(2,1)} %param.23, bf16[2048,1,704]{0,2,1:T(8,128)(2,1)S(1)} %get-tuple-element.303, bf16[2048,1,704]{0,2,1:T(8,128)(2,1)S(1)} %get-tuple-element.302), kind=kOutput, calls=%fused_computation.56 | convolution fusion | flops 11818237952 | bytes 19922944 | tf_op jit(solution)/shard_map/dot_general | solution.py:81
  382.8 71.6 %reduce-scatter.15.cloned.1.call-done = bf16[256,2048]{1,0:T(8,128)(2,1)} async-done(((bf16[2048,2048]{1,0:T(8,128)(2,1)}), bf16[256,2048]{1,0:T(8,128)(2,1)}) %reduce-scatter.15.cloned.1.call-update) | async-done | bytes 1048592 | tf_op jit(solution)/shard_map/reduce_scatter | solution.py:192
  461.6 54.3 %all-gather.11.cloned.1.call-done = bf16[2048,2048]{1,0:T(8,128)(2,1)} async-done(((bf16[256,2048]{1,0:T(8,128)(2,1)}), bf16[2048,2048]{1,0:T(8,128)(2,1)}) %all-gather.11.cloned.1.call-update) | async-done | bytes 8388624 | tf_op jit(solution)/shard_map/all_gather | solution.py:202
  515.9 7.0 convolution_convert_fusion.5
  531.4 245.9 %while.29 = (s32[]{:T(128)}, f32[2048,4,64]{0,2,1:T(8,128)}, f32[2048,4,64]{0,2,1:T(8,128)}, f32[4,512,4,64]{1,0,3,2:T(4,128)}, bf16[4,512,4,64]{1,3,2,0:T(8,128...) while((s32[]{:T(128)}, f32[2048,4,64]{0,2,1:T(8,128)}, ...), condition=%wide.region_17.18_spmd.clone, body=%wide.region_15.17_spmd.clone.sunk | while | flops 2753165312 | bytes 233386272 | solution.py:238
  536.5 5.7 copy-done.1
  542.2 7.1 fusion.163
  549.3 12.8 multiply_reduce_fusion.3
  562.1 12.2 multiply_convert_fusion.3
  581.5 11.1 dynamic_update_slice.22
  603.3 7.5 fusion.163
  610.8 12.8 multiply_reduce_fusion.3
  623.6 12.2 multiply_convert_fusion.3
  643.0 11.1 dynamic_update_slice.22
  664.8 7.5 fusion.163
  672.3 12.8 multiply_reduce_fusion.3
  685.1 12.2 multiply_convert_fusion.3
  704.5 11.1 dynamic_update_slice.22
  726.3 7.5 fusion.163
  733.8 12.8 multiply_reduce_fusion.3
  746.6 12.2 multiply_convert_fusion.3
  766.0 11.1 dynamic_update_slice.22
  788.6 9.2 convolution_convert_fusion
  804.6 9.1 convolution_convert_fusion.1
  813.8 11.4 convolution_convert_fusion.3
  825.2 16.2 %fusion.58 = bf16[2048,2,704]{0,2,1:T(8,128)(2,1)} fusion(bf16[2048,2048]{1,0:T(8,128)(2,1)} %all-gather.7.cloned.1.call-done, bf16[2048,1,704]{0,2,1:T(8,128)(2,1)S(1)} %copy-done.47, bf16[2048,1,704]{0,2,1:T(8,128)(2,1)S(1)} %copy-done.45), kind=kOutput, calls=%fused_computation.79 | convolution fusion | flops 11825577984 | bytes 19922944 | tf_op jit(solution)/shard_map/dot_general | solution.py:75
  842.9 11.6 fusion.66
  854.5 14.9 %reduce-scatter.17.cloned.1.call-done = bf16[256,2048]{1,0:T(8,128)(2,1)} async-done(((bf16[2048,2048]{1,0:T(8,128)(2,1)}), bf16[256,2048]{1,0:T(8,128)(2,1)}) %reduce-scatter.17.cloned.1.call-update) | async-done | bytes 1048592 | tf_op jit(solution)/shard_map/reduce_scatter | solution.py:257
  875.7 7.5 convolution_convert_fusion.4
  883.5 61.5 %reduce-scatter.13.cloned.1.call-done = bf16[256,2048]{1,0:T(8,128)(2,1)} async-done(((bf16[2048,2048]{1,0:T(8,128)(2,1)}), bf16[256,2048]{1,0:T(8,128)(2,1)}) %reduce-scatter.13.cloned.1.call-update) | async-done | bytes 1048592 | tf_op jit(solution)/shard_map/reduce_scatter | solution.py:173
  950.3 32.5 %reduce-scatter.19.cloned.1.call-done = bf16[256,2]{1,0:T(8,128)(2,1)} async-done(((bf16[2048,2]{1,0:T(8,128)(2,1)}), bf16[256,2]{1,0:T(8,128)(2,1)}) %reduce-scatter.19.cloned.1.call-update) | async-done | bytes 1040
  983.7 36.2 %reduce-scatter.21.cloned.1.call-done = bf16[256,2]{1,0:T(8,128)(2,1)} async-done(((bf16[2048,2]{1,0:T(8,128)(2,1)}), bf16[256,2]{1,0:T(8,128)(2,1)}) %reduce-scatter.21.cloned.1.call-update) | async-done | bytes 1040
  1020.8 11.9 all-reduce.1
  1035.0 423.0 %all-reduce.5.cloned.1.call-done = (bf16[2048,3,256]{2,0,1:T(8,128)(2,1)}, bf16[256,2048]{1,0:T(8,128)(2,1)}, bf16[2048,2,704]{0,2,1:T(8,128)(2,1)}, bf16[704,2048]{1,0:T(8,128)(2,1)}) async-done(((bf16[2048,3,256]{2,0,1:T(8,128)(2,1)}, bf16[256,2048]{1,0:T(8,128)(2,1)}, bf16[2048,2,704]{0,2,1:T(8,128)(2,1)}, bf16[704,2048]{1,0:T(8,128)(2,1)}), (bf16[2048,3,256]{2,0,1:T(8,128)(2,1)}, ...) | async-done | bytes 12845072 | tf_op jit(solution)/shard_map/psum | solution.py:282
  1468.0 6.0 convert_element_type.171
  (287 shorter events, 200.0 us)
Async XLA Ops:
  7.2 342.3 %copy-start = (bf16[704,2048]{1,0:T(8,128)(2,1)S(1)}, bf16[704,2048]{1,0:T(8,128)(2,1)}, u32[]{:S(2)}) copy-start(bf16[704,2048]{1,0:T(8,128)(2,1)} %param.24) | copy-start | bytes 8650756
  7.2 8.9 copy-start.42
  7.2 9.6 copy-start.18
  7.2 66.0 %all-gather.5.cloned.1.call-start = ((), (), s32[]{:S(2)}) async-start(), calls=%async_computation.6 | async-start | bytes 9437184 | tf_op jit(solution)/shard_map/all_gather | solution.py:113
  8.9 4.5 copy-start.31
  16.0 217.2 %reduce-scatter.11.cloned.1.call-start = ((), (), s32[]{:S(2)}) async-start(), calls=%async_computation.7 | async-start | bytes 9437184 | tf_op jit(solution)/shard_map/reduce_scatter | solution.py:157
  18.1 4.7 copy-start.43
  23.3 61.6 %copy-start.20 = (f32[2048,8]{0,1:T(8,128)}, f32[2048,8]{0,1:T(8,128)S(1)}, u32[]{:S(2)}) copy-start(f32[2048,8]{0,1:T(8,128)S(1)} %get-tuple-element.324) | copy-start | bytes 196612
  23.3 61.6 %copy-start.22 = (f32[2048,8]{0,1:T(8,128)}, f32[2048,8]{0,1:T(8,128)S(1)}, u32[]{:S(2)}) copy-start(f32[2048,8]{0,1:T(8,128)S(1)} %get-tuple-element.325) | copy-start | bytes 196612
  94.1 4.3 copy-start.7
  110.1 4.3 copy-start.7
  141.9 4.3 copy-start.7
  161.6 75.8 %copy-start.24 = (f32[1,2048]{1,0:T(1,128)S(1)}, f32[1,2048]{1,0:T(1,128)}, u32[]{:S(2)}) copy-start(f32[1,2048]{1,0:T(1,128)} %get-tuple-element.321) | copy-start | bytes 24580
  161.6 75.8 %copy-start.30 = (f32[1,2048]{1,0:T(1,128)S(1)}, f32[1,2048]{1,0:T(1,128)}, u32[]{:S(2)}) copy-start(f32[1,2048]{1,0:T(1,128)} %get-tuple-element.323) | copy-start | bytes 24580
  161.7 131.7 %all-gather.7.cloned.1.call-start = ((), (), s32[]{:S(2)}) async-start(), calls=%async_computation.8 | async-start | bytes 9437184 | tf_op jit(solution)/shard_map/all_gather | solution.py:164
  235.3 222.7 %copy-start.28 = (f32[256]{0:T(256)}, f32[256]{0:T(256)S(1)}, u32[]{:S(2)}) copy-start(f32[256]{0:T(256)S(1)} %broadcast_multiply_fusion.4) | copy-start | bytes 3076
  237.4 220.7 %copy-start.33 = (f32[256]{0:T(256)}, f32[256]{0:T(256)S(1)}, u32[]{:S(2)}) copy-start(f32[256]{0:T(256)S(1)} %add_rsqrt_fusion) | copy-start | bytes 3076
  239.0 110.4 %all-gather.9.cloned.1.call-start = ((), (), s32[]{:S(2)}) async-start(), calls=%async_computation.10 | async-start | bytes 9437184 | tf_op jit(solution)/shard_map/all_gather | solution.py:180
  239.6 214.8 %reduce-scatter.15.cloned.1.call-start = ((), (), s32[]{:S(2)}) async-start(), calls=%async_computation.11 | async-start | bytes 9437184 | tf_op jit(solution)/shard_map/reduce_scatter | solution.py:192
  382.8 133.1 %all-gather.11.cloned.1.call-start = ((), (), s32[]{:S(2)}) async-start(), calls=%async_computation.12 | async-start | bytes 9437184 | tf_op jit(solution)/shard_map/all_gather | solution.py:202
  461.5 407.9 %reduce-scatter.17.cloned.1.call-start = ((), (), s32[]{:S(2)}) async-start(), calls=%async_computation.13 | async-start | bytes 9437184 | tf_op jit(solution)/shard_map/reduce_scatter | solution.py:257
  536.4 5.7 copy-start.1
  562.1 12.2 copy-start.2
  597.5 5.7 copy-start.1
  623.6 12.2 copy-start.2
  659.0 5.7 copy-start.1
  685.1 12.2 copy-start.2
  720.5 5.7 copy-start.1
  746.5 12.2 copy-start.2
  777.3 5.2 copy-start.21
  777.3 5.2 copy-start.23
  797.8 147.2 %reduce-scatter.13.cloned.1.call-start = ((), (), s32[]{:S(2)}) async-start(), calls=%async_computation.9 | async-start | bytes 9437184 | tf_op jit(solution)/shard_map/reduce_scatter | solution.py:173
  813.7 169.1 %reduce-scatter.19.cloned.1.call-start = ((), (), s32[]{:S(2)}) async-start(), calls=%async_computation.14 | async-start | bytes 589824
  813.8 11.4 copy-start.45
  813.8 11.4 copy-start.47
  825.2 17.6 %copy-start.37 = (bf16[2048]{0:T(1024)(128)(2,1)S(1)}, bf16[2048]{0:T(1024)(128)(2,1)}, u32[]{:S(2)}) copy-start(bf16[2048]{0:T(1024)(128)(2,1)} %get-tuple-element.234) | copy-start | bytes 12292
  842.9 28.0 %copy-start.27 = (f32[1,2048]{1,0:T(1,128)S(1)}, f32[1,2048]{1,0:T(1,128)}, u32[]{:S(2)}) copy-start(f32[1,2048]{1,0:T(1,128)} %copy-done.26) | copy-start | bytes 24580
  842.9 28.0 %copy-start.32 = (f32[256]{0:T(256)S(1)}, f32[256]{0:T(256)}, u32[]{:S(2)}) copy-start(f32[256]{0:T(256)} %copy-done.31) | copy-start | bytes 3076
  842.9 28.0 %copy-start.36 = (f32[256]{0:T(256)S(1)}, f32[256]{0:T(256)}, u32[]{:S(2)}) copy-start(f32[256]{0:T(256)} %copy-done.35) | copy-start | bytes 3076
  874.5 145.4 %reduce-scatter.21.cloned.1.call-start = ((), (), s32[]{:S(2)}) async-start(), calls=%async_computation.15 | async-start | bytes 589824
  875.6 582.3 %all-reduce.5.cloned.1.call-start = ((), (), s32[]{:S(2)}) async-start(), calls=%async_computation.16 | async-start | bytes 25690112 | tf_op jit(solution)/shard_map/psum | solution.py:282
  883.2 61.7 %copy-start.25 = (f32[1,2048]{1,0:T(1,128)S(1)}, f32[1,2048]{1,0:T(1,128)}, u32[]{:S(2)}) copy-start(f32[1,2048]{1,0:T(1,128)} %get-tuple-element.321) | copy-start | bytes 24580
  883.2 61.7 %copy-start.29 = (f32[256]{0:T(256)S(1)}, f32[256]{0:T(256)}, u32[]{:S(2)}) copy-start(f32[256]{0:T(256)} %copy-done.28) | copy-start | bytes 3076
  883.2 61.7 %copy-start.34 = (f32[256]{0:T(256)S(1)}, f32[256]{0:T(256)}, u32[]{:S(2)}) copy-start(f32[256]{0:T(256)} %copy-done.33) | copy-start | bytes 3076
  883.2 61.7 %copy-start.39 = (f32[256]{0:T(256)S(1)}, f32[256]{0:T(256)}, u32[]{:S(2)}) copy-start(f32[256]{0:T(256)} %copy-done.38) | copy-start | bytes 3076
  883.2 61.7 %copy-start.41 = (f32[256]{0:T(256)S(1)}, f32[256]{0:T(256)}, u32[]{:S(2)}) copy-start(f32[256]{0:T(256)} %copy-done.40) | copy-start | bytes 3076
  1458.0 10.0 slice-start
  1460.9 7.1 slice-start.1
  (28 other events, 74.0 us)
Sparse Core Ops, SparseCore 0:
  16.2 56.9 all-gather.4
  161.8 71.4 reduce-scatter.10
  239.1 54.2 all-gather.6
  295.1 54.2 all-gather.8
  382.9 71.4 reduce-scatter.14
  461.6 54.2 all-gather.10
  797.9 71.4 reduce-scatter.16
  873.4 71.4 reduce-scatter.12
  948.6 34.1 reduce-scatter.18
  985.7 34.1 reduce-scatter.20
  1023.3 434.5 all-reduce.4
where the time goes:
time: 1490 us; the launch traced here: 1480 us
  waiting for transfers between devices  907 us (61%)
  matrix products  296 us (20%)
  other arithmetic  133 us (9%)
  local copies, waits for them, and re-layouts  116 us (8%)
    psum x1, waiting for transfers between devices, local(): lax.psum(grad_qkv.astype(jnp.bfloat16), 'dp').astype(jnp.float32)  423 us
    reduce_scatter x1, waiting for transfers between devices, local(): lax.psum_scatter(contract_cols(grad_pair, gate_matrix).astype(jnp.bfloat1...  71.6 us
    reduce_scatter x1, waiting for transfers between devices, local(): lax.psum_scatter(jnp.dot(attended, w_out, preferred_element_type=jnp.floa...  71.6 us
    unnamed x13, waiting for transfers between devices  69.3 us
    reduce_scatter x1, waiting for transfers between devices, local(): lax.psum_scatter(jnp.dot(activation, w_down, preferred_element_type=jnp.f...  61.5 us
    all_gather x1, waiting for transfers between devices, local(): lax.all_gather(grad_hidden.astype(jnp.bfloat16), 'tp', axis=0, tiled=True)  54.3 us
    all_gather x1, waiting for transfers between devices, local(): lax.all_gather(normed_two.astype(jnp.bfloat16), 'tp', axis=0, tiled=True)  53.8 us
    dot_general x4, matrix products, backward_block(): jnp.einsum('bhd,khd->hbk', grad_block, value_rows, preferred_element_type...  51.2 us
  transfers between devices with their start and end apart: 11, of which 11 were waited for; matrix products, arithmetic and copies ran while one was open for 7% of the time, Pallas kernels for 0%

commit v1 on v0

--- a/solution.py
+++ b/solution.py
@@ -8,6 +8,12 @@
 HEAD_DIM = 64
 ROT = 16
 EPSILON = 1e-05
+
+
+def joined_along(tiles, dim):
+    tiles = jnp.moveaxis(tiles, 0, dim)
+    dims = tiles.shape
+    return tiles.reshape(*dims[:dim], dims[dim] * dims[dim + 1], *dims[dim + 2 :])
 
 
 def norm_forward(values, gain, shift_bias):
@@ -177,7 +183,19 @@
         tiled=True,
     ).astype(jnp.float32)
     grad_float = out_grad.astype(jnp.float32)
-    portion = lax.all_gather(out_grad, "tp", axis=0, tiled=True)
+    size = lax.axis_size("tp")
+    pairs = [(i, (i + 1) % size) for i in range(size)]
+    back = [(b, a) for a, b in pairs]
+    lower, upper = ([], [])
+    for lap in range(size - 1):
+        if lap % 2 == 0:
+            lower.append(lax.ppermute(lower[-1] if lower else out_grad, "tp", pairs))
+        else:
+            upper.append(lax.ppermute(upper[-1] if upper else out_grad, "tp", back))
+    blocks_2 = jnp.stack([*lower[::-1], out_grad, *upper])
+    shift = lax.axis_index("tp") - len(lower)
+    blocks_2 = blocks_2[(jnp.arange(size) - shift) % size]
+    portion = joined_along(blocks_2, 0)
     weight_sum = contract_rows(activation, portion)
     grad_act = contract_cols(portion, w_down)
     grad_down, grad_act = (weight_sum, grad_act)

time: 1490 us -> 1540 us (1.034)
  local copies, waits for them, and re-layouts: 116 us -> 137 us
  waiting for transfers between devices: 907 us -> 925 us
    ppermute x0 -> x7, waiting for transfers between devices: none -> 109 us  [the longest x4 109 us: local(): lower.append(lax.ppermute(lower[-1] if lower else out_grad, 'tp', pairs))]
    all_gather x1, waiting for transfers between devices: 53.8 us -> 0.01 us  [local(): lax.all_gather(normed_two.astype(jnp.bfloat16), 'tp', axis=0, tiled=True)]
    all_gather x1 -> x0, waiting for transfers between devices: 37.2 us -> none  [local(): portion = lax.all_gather(out_grad, 'tp', axis=0, tiled=True)]
    unnamed x100 -> x113, local copies, waits for them, and re-layouts: 22.1 us -> 33.6 us
    unnamed x13 -> x12, waiting for transfers between devices: 69.3 us -> 68.9 us
  transfers between devices with their start and end apart: 11 -> 17, of which waited for: 11 -> 14; matrix products, arithmetic and copies ran while one was open for 7% -> 7% of each run, Pallas kernels for 0% -> 0%
where the time goes in v1:
time: 1540 us; the launch traced here: 1530 us
  waiting for transfers between devices  925 us (60%)
  matrix products  303 us (20%)
  local copies, waits for them, and re-layouts  137 us (9%)
  other arithmetic  129 us (8%)
    psum x1, waiting for transfers between devices, local(): lax.psum(grad_qkv.astype(jnp.bfloat16), 'dp').astype(jnp.float32)  423 us
    ppermute x4, waiting for transfers between devices, local(): lower.append(lax.ppermute(lower[-1] if lower else out_grad, 'tp', pairs))  109 us
    reduce_scatter x1, waiting for transfers between devices, local(): lax.psum_scatter(contract_cols(grad_pair, gate_matrix).astype(jnp.bfloat1...  73.1 us
    reduce_scatter x1, waiting for transfers between devices, local(): lax.psum_scatter(jnp.dot(attended, w_out, preferred_element_type=jnp.floa...  71.6 us
    unnamed x12, waiting for transfers between devices  68.9 us
    reduce_scatter x1, waiting for transfers between devices, local(): lax.psum_scatter(jnp.dot(activation, w_down, preferred_element_type=jnp.f...  60.7 us
    all_gather x1, waiting for transfers between devices, local(): lax.all_gather(grad_hidden.astype(jnp.bfloat16), 'tp', axis=0, tiled=True)  54.3 us
    dot_general x4, matrix products, backward_block(): jnp.einsum('bhd,khd->hbk', grad_block, value_rows, preferred_element_type...  51.3 us
  transfers between devices with their start and end apart: 17, of which 14 were waited for; matrix products, arithmetic and copies ran while one was open for 7% of the time, Pallas kernels for 0%

profile of v1, /device:TPU:0, one launch (start us, length us, event | category | flops | bytes accessed | tf_op | source)
XLA Modules:
  0.0 1532.0 jit_solution(3001224195510212642)
XLA Ops:
  23.3 49.9 %all-gather.4.cloned.1.call-done = bf16[2048,2048]{1,0:T(8,128)(2,1)} async-done(((bf16[256,2048]{1,0:T(8,128)(2,1)}), bf16[2048,2048]{1,0:T(8,128)(2,1)}) %all-gather.4.cloned.1.call-update) | async-done | bytes 8388624 | tf_op jit(solution)/shard_map/all_gather | solution.py:119
  73.2 10.1 fusion.70
  88.5 63.9 %while.28 = (s32[]{:T(128)}, bf16[4,512,4,64]{1,3,2,0:T(8,128)(2,1)}, f32[4,4,512]{2,1,0:T(4,128)S(1)}, s32[4,512]{1,0:T(4,128)S(1)}, s32[1,2048]{1,0:T(1,128)S(...) while((s32[]{:T(128)}, ...), condition=%wide.region_7.8_spmd.clone, body=%wide.region_4.7_spmd.clone.sunk | while | flops 1127348224 | bytes 61427864 | solution.py:161
  98.4 5.9 fusion.161
  114.4 5.9 fusion.161
  146.2 5.9 fusion.161
  161.6 71.6 %reduce-scatter.11.cloned.1.call-done = bf16[256,2048]{1,0:T(8,128)(2,1)} async-done(((bf16[2048,2048]{1,0:T(8,128)(2,1)}), bf16[256,2048]{1,0:T(8,128)(2,1)}) %reduce-scatter.11.cloned.1.call-update) | async-done | bytes 1048592 | tf_op jit(solution)/shard_map/reduce_scatter | solution.py:163
  239.1 23.0 %collective-permute-done = bf16[256,2048]{1,0:T(8,128)(2,1)S(1)} collective-permute-done((bf16[256,2048]{1,0:T(8,128)(2,1)}, bf16[256,2048]{1,0:T(8,128)(2,1)S(1)}, u32[]{:S(2)}, u32[]{:S(2)}) %collective-permute-start) | collective-permute-done | bytes 1048608 | tf_op jit(solution)/shard_map/ppermute | solution.py:192
  265.7 38.6 %collective-permute-done.1 = bf16[256,2048]{1,0:T(8,128)(2,1)S(1)} collective-permute-done((bf16[256,2048]{1,0:T(8,128)(2,1)S(1)}, bf16[256,2048]{1,0:T(8,128)(2,1)S(1)}, u32[]{:S(2)}, u32[]{:S(2)}) %collective-permute-start.1) | collective-permute-done | bytes 1048608 | tf_op jit(solution)/shard_map/ppermute | solution.py:192
  310.3 24.2 %collective-permute-done.2 = bf16[256,2048]{1,0:T(8,128)(2,1)} collective-permute-done((bf16[256,2048]{1,0:T(8,128)(2,1)S(1)}, bf16[256,2048]{1,0:T(8,128)(2,1)}, u32[]{:S(2)}, u32[]{:S(2)}) %collective-permute-start.2) | collective-permute-done | bytes 1048608 | tf_op jit(solution)/shard_map/ppermute | solution.py:192
  337.2 23.1 %collective-permute-done.3 = bf16[256,2048]{1,0:T(8,128)(2,1)} collective-permute-done((bf16[256,2048]{1,0:T(8,128)(2,1)}, bf16[256,2048]{1,0:T(8,128)(2,1)}, u32[]{:S(2)}, u32[]{:S(2)}) %collective-permute-start.3) | collective-permute-done | bytes 1048608 | tf_op jit(solution)/shard_map/ppermute | solution.py:192
  373.7 8.3 gather_fusion
  382.0 19.0 %fusion.53 = f32[2048,2,704]{0,2,1:T(8,128)} fusion(bf16[2048,2048]{1,0:T(8,128)(2,1)} %all-gather.6.cloned.1.call-done, bf16[2048,2,704]{0,2,1:T(8,128)(2,1)} %param.23), kind=kOutput, calls=%fused_computation.65 | convolution fusion | flops 11811160064 | bytes 25690112 | tf_op jit(solution)/shard_map/dot_general | solution.py:171
  400.9 12.2 fusion.60
  414.8 17.6 %bitcast_convert_fusion = bf16[2048,2048]{1,0:T(8,128)(2,1)} fusion(bf16[2048,2,704]{0,2,1:T(8,128)(2,1)S(1)} %bitcast.303, bf16[2048,1,704]{0,2,1:T(8,128)(2,1)} %get-tuple-element.303, bf16[2048,1,704]{0,2,1:T(8,128)(2,1)S(1)} %get-tuple-element.302), kind=kOutput, calls=%fused_computation.57 | convolution fusion | flops 11818237952 | bytes 19922944 | tf_op jit(solution)/shard_map/dot_general | solution.py:87
  432.5 73.1 %reduce-scatter.15.cloned.1.call-done = bf16[256,2048]{1,0:T(8,128)(2,1)} async-done(((bf16[2048,2048]{1,0:T(8,128)(2,1)}), bf16[256,2048]{1,0:T(8,128)(2,1)}) %reduce-scatter.15.cloned.1.call-update) | async-done | bytes 1048592 | tf_op jit(solution)/shard_map/reduce_scatter | solution.py:210
  513.5 54.3 %all-gather.8.cloned.1.call-done = bf16[2048,2048]{1,0:T(8,128)(2,1)} async-done(((bf16[256,2048]{1,0:T(8,128)(2,1)}), bf16[2048,2048]{1,0:T(8,128)(2,1)}) %all-gather.8.cloned.1.call-update) | async-done | bytes 8388624 | tf_op jit(solution)/shard_map/all_gather | solution.py:220
  567.8 7.0 convolution_convert_fusion.5
  583.3 246.0 %while.29 = (s32[]{:T(128)}, f32[2048,4,64]{0,2,1:T(8,128)}, f32[2048,4,64]{0,2,1:T(8,128)}, f32[4,512,4,64]{1,0,3,2:T(4,128)}, bf16[4,512,4,64]{1,3,2,0:T(8,128...) while((s32[]{:T(128)}, f32[2048,4,64]{0,2,1:T(8,128)}, ...), condition=%wide.region_17.18_spmd.clone, body=%wide.region_15.17_spmd.clone.sunk | while | flops 2753165312 | bytes 233386272 | solution.py:256
  594.1 7.1 fusion.174
  601.2 12.8 multiply_reduce_fusion.3
  614.0 12.2 multiply_convert_fusion.4
  633.5 11.1 dynamic_update_slice.22
  655.2 7.5 fusion.174
  662.7 12.8 multiply_reduce_fusion.3
  675.5 12.2 multiply_convert_fusion.4
  695.0 11.1 dynamic_update_slice.22
  716.7 7.5 fusion.174
  724.2 12.8 multiply_reduce_fusion.3
  737.0 12.2 multiply_convert_fusion.4
  756.5 11.1 dynamic_update_slice.22
  778.2 7.5 fusion.174
  785.7 12.8 multiply_reduce_fusion.3
  798.5 12.2 multiply_convert_fusion.4
  818.0 11.1 dynamic_update_slice.22
  840.2 9.1 convolution_convert_fusion
  849.4 13.8 convolution_convert_fusion.1
  863.3 14.1 convolution_convert_fusion.3
  877.4 16.2 %fusion.65 = bf16[2048,2,704]{0,2,1:T(8,128)(2,1)} fusion(bf16[2048,2048]{1,0:T(8,128)(2,1)} %all-gather.6.cloned.1.call-done, bf16[2048,1,704]{0,2,1:T(8,128)(2,1)S(1)} %copy-done.48, bf16[2048,1,704]{0,2,1:T(8,128)(2,1)S(1)} %copy-done.47), kind=kOutput, calls=%fused_computation.88 | convolution fusion | flops 11825577984 | bytes 19922944 | tf_op jit(solution)/shard_map/dot_general | solution.py:81
  895.1 11.5 fusion.73
  906.7 14.4 reduce-scatter.17.cloned.1.call-done
  927.3 7.7 convolution_convert_fusion.4
  935.3 60.7 %reduce-scatter.13.cloned.1.call-done = bf16[256,2048]{1,0:T(8,128)(2,1)} async-done(((bf16[2048,2048]{1,0:T(8,128)(2,1)}), bf16[256,2048]{1,0:T(8,128)(2,1)}) %reduce-scatter.13.cloned.1.call-update) | async-done | bytes 1048592 | tf_op jit(solution)/shard_map/reduce_scatter | solution.py:179
  1001.4 32.4 %reduce-scatter.19.cloned.1.call-done = bf16[256,2]{1,0:T(8,128)(2,1)} async-done(((bf16[2048,2]{1,0:T(8,128)(2,1)}), bf16[256,2]{1,0:T(8,128)(2,1)}) %reduce-scatter.19.cloned.1.call-update) | async-done | bytes 1040
  1034.7 36.3 %reduce-scatter.21.cloned.1.call-done = bf16[256,2]{1,0:T(8,128)(2,1)} async-done(((bf16[2048,2]{1,0:T(8,128)(2,1)}), bf16[256,2]{1,0:T(8,128)(2,1)}) %reduce-scatter.21.cloned.1.call-update) | async-done | bytes 1040
  1071.9 11.9 all-reduce.1
  1086.2 422.8 %all-reduce.5.cloned.1.call-done = (bf16[2048,3,256]{2,0,1:T(8,128)(2,1)}, bf16[256,2048]{1,0:T(8,128)(2,1)}, bf16[2048,2,704]{0,2,1:T(8,128)(2,1)}, bf16[704,2048]{1,0:T(8,128)(2,1)}) async-done(((bf16[2048,3,256]{2,0,1:T(8,128)(2,1)}, bf16[256,2048]{1,0:T(8,128)(2,1)}, bf16[2048,2,704]{0,2,1:T(8,128)(2,1)}, bf16[704,2048]{1,0:T(8,128)(2,1)}), (bf16[2048,3,256]{2,0,1:T(8,128)(2,1)}, ...) | async-done | bytes 12845072 | tf_op jit(solution)/shard_map/psum | solution.py:300
  1519.0 6.0 convert_element_type.176
  (315 shorter events, 235.3 us)
Async XLA Ops:
  7.2 393.8 %copy-start = (bf16[704,2048]{1,0:T(8,128)(2,1)S(1)}, bf16[704,2048]{1,0:T(8,128)(2,1)}, u32[]{:S(2)}) copy-start(bf16[704,2048]{1,0:T(8,128)(2,1)} %param.24) | copy-start | bytes 8650756
  7.2 66.0 %all-gather.4.cloned.1.call-start = ((), (), s32[]{:S(2)}) async-start(), calls=%async_computation.6 | async-start | bytes 9437184 | tf_op jit(solution)/shard_map/all_gather | solution.py:119
  16.0 217.2 %reduce-scatter.11.cloned.1.call-start = ((), (), s32[]{:S(2)}) async-start(), calls=%async_computation.7 | async-start | bytes 9437184 | tf_op jit(solution)/shard_map/reduce_scatter | solution.py:163
  23.3 61.6 %copy-start.22 = (f32[2048,8]{0,1:T(8,128)}, f32[2048,8]{0,1:T(8,128)S(1)}, u32[]{:S(2)}) copy-start(f32[2048,8]{0,1:T(8,128)S(1)} %get-tuple-element.324) | copy-start | bytes 196612
  23.3 61.6 %copy-start.24 = (f32[2048,8]{0,1:T(8,128)}, f32[2048,8]{0,1:T(8,128)S(1)}, u32[]{:S(2)}) copy-start(f32[2048,8]{0,1:T(8,128)S(1)} %get-tuple-element.325) | copy-start | bytes 196612
  161.6 75.8 %copy-start.26 = (f32[1,2048]{1,0:T(1,128)S(1)}, f32[1,2048]{1,0:T(1,128)}, u32[]{:S(2)}) copy-start(f32[1,2048]{1,0:T(1,128)} %get-tuple-element.321) | copy-start | bytes 24580
  161.6 75.8 %copy-start.32 = (f32[1,2048]{1,0:T(1,128)S(1)}, f32[1,2048]{1,0:T(1,128)}, u32[]{:S(2)}) copy-start(f32[1,2048]{1,0:T(1,128)} %get-tuple-element.323) | copy-start | bytes 24580
  161.6 220.4 %all-gather.6.cloned.1.call-start = ((), (), s32[]{:S(2)}) async-start(), calls=%async_computation.8 | async-start | bytes 9437184 | tf_op jit(solution)/shard_map/all_gather | solution.py:170
  235.3 273.8 %copy-start.30 = (f32[256]{0:T(256)}, f32[256]{0:T(256)S(1)}, u32[]{:S(2)}) copy-start(f32[256]{0:T(256)S(1)} %broadcast_multiply_fusion.4) | copy-start | bytes 3076
  237.3 271.8 %copy-start.35 = (f32[256]{0:T(256)}, f32[256]{0:T(256)S(1)}, u32[]{:S(2)}) copy-start(f32[256]{0:T(256)S(1)} %add_rsqrt_fusion) | copy-start | bytes 3076
  238.9 266.7 %reduce-scatter.15.cloned.1.call-start = ((), (), s32[]{:S(2)}) async-start(), calls=%async_computation.10 | async-start | bytes 9437184 | tf_op jit(solution)/shard_map/reduce_scatter | solution.py:210
  239.0 23.1 %collective-permute-start = (bf16[256,2048]{1,0:T(8,128)(2,1)}, bf16[256,2048]{1,0:T(8,128)(2,1)S(1)}, u32[]{:S(2)}, u32[]{:S(2)}) collective-permute-start(bf16[256,2048]{1,0:T(8,128)(2,1)} %param.25), channel_id=1, source_target_pairs={{0,1},{1,2},{2,3},{3,4},{4,5},{5,6},{6,7},{7,0},{8,9},{9,10},{10,1... | collective-permute-start | bytes 3145736 | tf_op jit(solution)/shard_map/ppermute | solution.py:192
  263.1 41.3 %collective-permute-start.1 = (bf16[256,2048]{1,0:T(8,128)(2,1)S(1)}, bf16[256,2048]{1,0:T(8,128)(2,1)S(1)}, u32[]{:S(2)}, u32[]{:S(2)}) collective-permute-start(bf16[256,2048]{1,0:T(8,128)(2,1)S(1)} %collective-permute-done), channel_id=1, source_target_pairs={{0,1},{1,2},{2,3},{3,4},{4,5},{5,6},{6,7},{7,0},{8,9},{9,10},{10,1... | collective-permute-start | bytes 3145736 | tf_op jit(solution)/shard_map/ppermute | solution.py:192
  263.7 43.7 %collective-permute-start.4 = (bf16[256,2048]{1,0:T(8,128)(2,1)}, bf16[256,2048]{1,0:T(8,128)(2,1)}, u32[]{:S(2)}, u32[]{:S(2)}) collective-permute-start(bf16[256,2048]{1,0:T(8,128)(2,1)} %param.25), channel_id=1, source_target_pairs={{1,0},{2,1},{3,2},{4,3},{5,4},{6,5},{7,6},{0,7},{9,8},{10,9},{11,1... | collective-permute-start | bytes 3145736 | tf_op jit(solution)/shard_map/ppermute | solution.py:194
  305.3 29.2 %collective-permute-start.2 = (bf16[256,2048]{1,0:T(8,128)(2,1)S(1)}, bf16[256,2048]{1,0:T(8,128)(2,1)}, u32[]{:S(2)}, u32[]{:S(2)}) collective-permute-start(bf16[256,2048]{1,0:T(8,128)(2,1)S(1)} %collective-permute-done.1), channel_id=1, source_target_pairs={{0,1},{1,2},{2,3},{3,4},{4,5},{5,6},{6,7},{7,0},{8,9},{9,10},{10,1... | collective-permute-start | bytes 3145736 | tf_op jit(solution)/shard_map/ppermute | solution.py:192
  307.5 27.0 %collective-permute-start.5 = (bf16[256,2048]{1,0:T(8,128)(2,1)}, bf16[256,2048]{1,0:T(8,128)(2,1)}, u32[]{:S(2)}, u32[]{:S(2)}) collective-permute-start(bf16[256,2048]{1,0:T(8,128)(2,1)} %collective-permute-done.4), channel_id=1, source_target_pairs={{1,0},{2,1},{3,2},{4,3},{5,4},{6,5},{7,6},{0,7},{9,8},{10,9},{11,1... | collective-permute-start | bytes 3145736 | tf_op jit(solution)/shard_map/ppermute | solution.py:194
  334.5 25.9 %collective-permute-start.3 = (bf16[256,2048]{1,0:T(8,128)(2,1)}, bf16[256,2048]{1,0:T(8,128)(2,1)}, u32[]{:S(2)}, u32[]{:S(2)}) collective-permute-start(bf16[256,2048]{1,0:T(8,128)(2,1)} %collective-permute-done.2), channel_id=1, source_target_pairs={{0,1},{1,2},{2,3},{3,4},{4,5},{5,6},{6,7},{7,0},{8,9},{9,10},{10,1... | collective-permute-start | bytes 3145736 | tf_op jit(solution)/shard_map/ppermute | solution.py:192
  334.5 30.5 %copy-start.21 = (bf16[256,2048]{1,0:T(8,128)(2,1)S(1)}, bf16[256,2048]{1,0:T(8,128)(2,1)}, u32[]{:S(2)}) copy-start(bf16[256,2048]{1,0:T(8,128)(2,1)} %copy-done.20) | copy-start | bytes 3145732
  334.5 31.5 %copy-start.19 = (bf16[256,2048]{1,0:T(8,128)(2,1)S(1)}, bf16[256,2048]{1,0:T(8,128)(2,1)}, u32[]{:S(2)}) copy-start(bf16[256,2048]{1,0:T(8,128)(2,1)} %copy-done.18) | copy-start | bytes 3145732
  334.5 32.5 %copy-start.8 = (bf16[256,2048]{1,0:T(8,128)(2,1)S(1)}, bf16[256,2048]{1,0:T(8,128)(2,1)}, u32[]{:S(2)}) copy-start(bf16[256,2048]{1,0:T(8,128)(2,1)} %param.25) | copy-start | bytes 3145732
  334.5 38.1 %collective-permute-start.6 = (bf16[256,2048]{1,0:T(8,128)(2,1)}, bf16[256,2048]{1,0:T(8,128)(2,1)S(1)}, u32[]{:S(2)}, u32[]{:S(2)}) collective-permute-start(bf16[256,2048]{1,0:T(8,128)(2,1)} %collective-permute-done.5), channel_id=1, source_target_pairs={{1,0},{2,1},{3,2},{4,3},{5,4},{6,5},{7,6},{0,7},{9,8},{10,9},{11,1... | collective-permute-start | bytes 3145736 | tf_op jit(solution)/shard_map/ppermute | solution.py:194
  382.0 19.0 %copy-start.9 = (bf16[8,256,2048]{2,1,0:T(8,128)(2,1)S(1)}, bf16[8,256,2048]{2,1,0:T(8,128)(2,1)}, u32[]{:S(2)}) copy-start(bf16[8,256,2048]{2,1,0:T(8,128)(2,1)} %gather_fusion) | copy-start | bytes 25165828
  382.0 32.8 %slice-start.2 = ((s8[5767168]{0:T(1024)(128)(4,1)}), s8[4194304]{0:T(1024)(128)(4,1)S(1)}, s32[]{:S(2)}) async-start(s8[5767168]{0:T(1024)(128)(4,1)} %bitcast.302), calls=%async_computation.18 | async-start | bytes 8388608
  400.9 13.8 slice-start.3
  432.4 135.4 %all-gather.8.cloned.1.call-start = ((), (), s32[]{:S(2)}) async-start(), calls=%async_computation.11 | async-start | bytes 9437184 | tf_op jit(solution)/shard_map/all_gather | solution.py:220
  509.1 65.7 %copy-start.40 = (f32[256]{0:T(256)}, f32[256]{0:T(256)S(1)}, u32[]{:S(2)}) copy-start(f32[256]{0:T(256)S(1)} %get-tuple-element.329) | copy-start | bytes 3076
  509.1 65.7 %copy-start.42 = (f32[256]{0:T(256)}, f32[256]{0:T(256)S(1)}, u32[]{:S(2)}) copy-start(f32[256]{0:T(256)S(1)} %get-tuple-element.330) | copy-start | bytes 3076
  513.4 407.6 %reduce-scatter.17.cloned.1.call-start = ((), (), s32[]{:S(2)}) async-start(), calls=%async_computation.12 | async-start | bytes 9437184 | tf_op jit(solution)/shard_map/reduce_scatter | solution.py:275
  614.0 12.2 copy-start.2
  675.5 12.2 copy-start.2
  737.0 12.2 copy-start.2
  798.5 12.2 copy-start.2
  849.4 146.6 %reduce-scatter.13.cloned.1.call-start = ((), (), s32[]{:S(2)}) async-start(), calls=%async_computation.9 | async-start | bytes 9437184 | tf_op jit(solution)/shard_map/reduce_scatter | solution.py:179
  863.3 170.5 %reduce-scatter.19.cloned.1.call-start = ((), (), s32[]{:S(2)}) async-start(), calls=%async_computation.13 | async-start | bytes 589824
  863.3 14.1 copy-start.47
  863.3 14.1 copy-start.48
  877.4 17.7 %copy-start.39 = (bf16[2048]{0:T(1024)(128)(2,1)S(1)}, bf16[2048]{0:T(1024)(128)(2,1)}, u32[]{:S(2)}) copy-start(bf16[2048]{0:T(1024)(128)(2,1)} %get-tuple-element.234) | copy-start | bytes 12292
  895.1 27.3 %copy-start.29 = (f32[1,2048]{1,0:T(1,128)S(1)}, f32[1,2048]{1,0:T(1,128)}, u32[]{:S(2)}) copy-start(f32[1,2048]{1,0:T(1,128)} %copy-done.28) | copy-start | bytes 24580
  895.1 27.3 %copy-start.34 = (f32[256]{0:T(256)S(1)}, f32[256]{0:T(256)}, u32[]{:S(2)}) copy-start(f32[256]{0:T(256)} %copy-done.33) | copy-start | bytes 3076
  895.1 27.3 %copy-start.38 = (f32[256]{0:T(256)S(1)}, f32[256]{0:T(256)}, u32[]{:S(2)}) copy-start(f32[256]{0:T(256)} %copy-done.37) | copy-start | bytes 3076
  926.1 144.9 %reduce-scatter.21.cloned.1.call-start = ((), (), s32[]{:S(2)}) async-start(), calls=%async_computation.14 | async-start | bytes 589824
  927.2 581.8 %all-reduce.5.cloned.1.call-start = ((), (), s32[]{:S(2)}) async-start(), calls=%async_computation.15 | async-start | bytes 25690112 | tf_op jit(solution)/shard_map/psum | solution.py:300
  935.0 61.0 %copy-start.27 = (f32[1,2048]{1,0:T(1,128)S(1)}, f32[1,2048]{1,0:T(1,128)}, u32[]{:S(2)}) copy-start(f32[1,2048]{1,0:T(1,128)} %get-tuple-element.321) | copy-start | bytes 24580
  935.0 61.0 %copy-start.31 = (f32[256]{0:T(256)S(1)}, f32[256]{0:T(256)}, u32[]{:S(2)}) copy-start(f32[256]{0:T(256)} %copy-done.30) | copy-start | bytes 3076
  935.0 61.0 %copy-start.36 = (f32[256]{0:T(256)S(1)}, f32[256]{0:T(256)}, u32[]{:S(2)}) copy-start(f32[256]{0:T(256)} %copy-done.35) | copy-start | bytes 3076
  935.0 61.0 %copy-start.41 = (f32[256]{0:T(256)S(1)}, f32[256]{0:T(256)}, u32[]{:S(2)}) copy-start(f32[256]{0:T(256)} %copy-done.40) | copy-start | bytes 3076
  935.0 61.0 %copy-start.43 = (f32[256]{0:T(256)S(1)}, f32[256]{0:T(256)}, u32[]{:S(2)}) copy-start(f32[256]{0:T(256)} %copy-done.42) | copy-start | bytes 3076
  1509.0 10.0 slice-start
  (37 other events, 139.9 us)
Sparse Core Ops, SparseCore 0:
  16.2 56.9 all-gather.3
  161.7 71.4 reduce-scatter.10
  239.1 76.9 all-gather.5
  432.5 73.0 reduce-scatter.14
  513.5 54.2 all-gather.7
  849.5 71.4 reduce-scatter.16
  924.5 71.4 reduce-scatter.12
  999.6 34.1 reduce-scatter.18
  1036.9 34.0 reduce-scatter.20
  1074.3 434.6 all-reduce.4
